TPU v7x, 32 devices: a whole 2x2x4 slice. The times are simulated.
32 devices in a mesh: row: 2 (over y), col: 8 (over z, x), layer: 2 (over core).
Axes of the slice: x: 2, y: 2, z: 4, core: 2. Of those that a mesh axis runs over, the one named last changes fastest.
Arguments:
- anomaly_x: bfloat16 [8, 4096, 4096], P(None, 'row', ('layer', 'col')), may hold values from -0.09375 to 0.09375
- anomaly_y: bfloat16 [8, 4096, 4096], P(None, 'col', ('layer', 'row')), may hold values from -6 to 6
Outputs:
- covariance: bfloat16 [8, 4096, 4096], P('layer', 'row', 'col')
All inputs are finite; a program needn't handle non-finite values.
Results may differ from a plain program's by a relative error of at most 0.001.
Values may be sent and summed in bfloat16 or wider, within the bound.
A program may use at most 192 MiB of HBM per device.

v0:
```python
import jax
import jax.numpy as jnp
from jax import lax
from jax.sharding import PartitionSpec as P


def on_device(anomaly_x, anomaly_y):
    panel_x = lax.all_gather(anomaly_x, "col", axis=2, tiled=True)
    partial_tile = jnp.einsum(
        "bik,bjk->bij",
        panel_x,
        lax.all_gather(anomaly_y, "row", axis=2, tiled=True),
        preferred_element_type=jnp.float32,
    )
    summed = lax.psum_scatter(partial_tile, "layer", scatter_dimension=0, tiled=True)
    return summed.astype(jnp.bfloat16)


def solution(mesh):
    placed = (P(None, "row", ("layer", "col")), P(None, "col", ("layer", "row")))
    return jax.shard_map(
        on_device, mesh=mesh, in_specs=placed, out_specs=P("layer", "row", "col"), check_vma=False
    )
```

profile of v0, /device:TPU:9, one launch (start us, length us, event | category | flops | bytes accessed | tf_op | source)
XLA Modules:
  0.0 1586.4 jit_solution(16807389690178058107)
XLA Ops:
  6.5 0.0 all-gather.5.cloned.1.call-start
  6.5 0.7 all-gather.5.cloned.1.call-update
  7.3 0.0 all-gather.3.cloned.1.call-start
  7.3 0.7 all-gather.3.cloned.1.call-update
  8.0 0.0 reduce-scatter.2.cloned.1.call-start
  8.1 200.7 %all-gather.5.cloned.1.call-done = bf16[8,512,2048]{2,1,0:T(8,128)(2,1)} async-done(((bf16[8,512,1024]{2,1,0:T(8,128)(2,1)}), bf16[8,512,2048]{2,1,0:T(8,128)(2,1)}) %all-gather.5.cloned.1.call-update) | async-done | bytes 16777232 | tf_op jit(solution)/shard_map/all_gather | solution.py:12
  208.8 1269.7 %all-gather.3.cloned.1.call-done = bf16[8,2048,2048]{2,1,0:T(8,128)(2,1)} async-done(((bf16[8,2048,256]{2,1,0:T(8,128)(2,1)}), bf16[8,2048,2048]{2,1,0:T(8,128)(2,1)}) %all-gather.3.cloned.1.call-update) | async-done | bytes 67108880 | tf_op jit(solution)/shard_map/all_gather | solution.py:8
  1478.5 49.1 %fusion = f32[8,2048,512]{2,1,0:T(8,128)} fusion(bf16[8,2048,2048]{2,1,0:T(8,128)(2,1)} %all-gather.3.cloned.1.call-done, bf16[8,512,2048]{2,1,0:T(8,128)(2,1)} %all-gather.5.cloned.1.call-done), kind=kOutput, calls=%fused_computation | convolution fusion | flops 34359738368 | bytes 117440512 | tf_op jit(solution)/shard_map/bik,bjk->bij/dot_general | solution.py:9
  1527.6 0.0 reduce-scatter.2.cloned.1.call-update
  1527.6 43.3 %reduce-scatter.2.cloned.1.call-done = f32[4,2048,512]{2,1,0:T(8,128)} async-done(((f32[8,2048,512]{2,1,0:T(8,128)}), f32[4,2048,512]{2,1,0:T(8,128)}) %reduce-scatter.2.cloned.1.call-update) | async-done | bytes 16777232 | tf_op jit(solution)/shard_map/reduce_scatter | solution.py:15
  1570.9 9.0 convert_element_type.3
Async XLA Ops:
  6.5 202.2 %all-gather.5.cloned.1.call-start = ((), (), s32[]{:S(2)}) async-start(), calls=%async_computation.2 | async-start | bytes 25165824 | tf_op jit(solution)/shard_map/all_gather | solution.py:12
  7.3 1471.2 %all-gather.3.cloned.1.call-start = ((), (), s32[]{:S(2)}) async-start(), calls=%async_computation.1 | async-start | bytes 75497472 | tf_op jit(solution)/shard_map/all_gather | solution.py:8
  8.0 1562.9 %reduce-scatter.2.cloned.1.call-start = ((), (), s32[]{:S(2)}) async-start(), calls=%async_computation.3 | async-start | bytes 50331648 | tf_op jit(solution)/shard_map/reduce_scatter | solution.py:15
Sparse Core Ops, SparseCore 0:
  8.9 199.8 all-gather.4
  210.2 1268.2 all-gather.2
  1527.7 43.1 reduce-scatter.1
where the time goes:
time: 1590 us
  waiting for transfers between devices  1520 us (96%)
  matrix products  49.1 us (3%)
    all_gather x1, waiting for transfers between devices, on_device(): panel_x = lax.all_gather(anomaly_x, 'col', axis=2, tiled=True)  1270 us
    all_gather x1, waiting for transfers between devices, on_device(): lax.all_gather(anomaly_y, 'row', axis=2, tiled=True)  201 us
    dot_general x1, matrix products, on_device(): jnp.einsum('bik,bjk->bij', panel_x, lax.all_gather(anomaly_y, 'row', axis...  49.1 us
    reduce_scatter x1, waiting for transfers between devices, on_device(): lax.psum_scatter(partial_tile, 'layer', scatter_dimension=0, tiled=True)  43.3 us
  transfers between devices with their start and end apart: 3, of which 3 were waited for; matrix products, arithmetic and copies ran while one was open for 0% of the time, Pallas kernels for 0%

commit v1 on v0

v1 whole, which is shorter than its diff:
```python
import functools

import jax
import jax.numpy as jnp
from jax import lax
from jax.experimental import pallas as pl
from jax.experimental.pallas import tpu as pltpu
from jax.sharding import PartitionSpec as P

LANES = 128
MESH = pl.DeviceIdType.MESH
NT = (((1,), (1,)), ((), ()))


def gathered(anomaly_x, anomaly_y):
    panel_x = lax.all_gather(anomaly_x, "col", axis=2, tiled=True)
    partial_tile = jnp.einsum(
        "bik,bjk->bij",
        panel_x,
        lax.all_gather(anomaly_y, "row", axis=2, tiled=True),
        preferred_element_type=jnp.float32,
    )
    summed = lax.psum_scatter(partial_tile, "layer", scatter_dimension=0, tiled=True)
    return summed.astype(jnp.bfloat16)


def kernel(
    sizes, x_ref, y_ref, o_ref, xg, yg, og, rx, ry, ro, local_sem,
    x_send, x_recv, xf_send, xf_recv, y_send, y_recv, yf_send, yf_recv,
    r_send, r_recv, q_send, o_send, o_recv, op_send, op_recv, oq_send,
):
    rows, planes, lines, layers = sizes
    y, col, c = lax.axis_index("row"), lax.axis_index("col"), lax.axis_index("layer")
    z, x = col // lines, lax.rem(col, lines)
    depth_x, depth_y = x_ref.shape[2], y_ref.shape[2]
    height, width = x_ref.shape[1], y_ref.shape[1]
    group = depth_x * planes * lines
    relayed = planes == 4
    half = height // 2

    def plane(d):
        return lax.rem(z + d + planes, planes)

    def core(e):
        return lax.rem(c + e + layers, layers)

    def dev(yy, zz, xx, cc):
        return {"row": yy, "col": zz * lines + xx, "layer": cc}

    def xcols(cc, zz, xx):
        return pl.ds(pl.multiple_of(cc * group + (zz * lines + xx) * depth_x, depth_x), depth_x)

    def ycols(cc, yy):
        return pl.ds(pl.multiple_of(cc * group + yy * depth_y, depth_y), depth_y)

    def batch(zz, cc):
        return cc * planes + zz

    xline = [lax.rem(x + d, lines) for d in range(1, lines)]
    yline = [lax.rem(y + d, rows) for d in range(1, rows)]
    peers = [dev(y, plane(d), x, core(e)) for d in range(planes) for e in range(layers) if d or e]
    peers += [dev(y, z, xx, c) for xx in xline] + [dev(yy, z, x, c) for yy in yline]
    barrier = pltpu.get_barrier_semaphore()
    for peer in peers:
        pl.semaphore_signal(barrier, inc=1, device_id=peer, device_id_type=MESH)
    pl.semaphore_wait(barrier, len(peers))

    sent = []

    def push(src, dst, s, r, to):
        cp = pltpu.make_async_remote_copy(
            src_ref=src, dst_ref=dst, send_sem=s, recv_sem=r, device_id=to, device_id_type=MESH
        )
        cp.start()
        sent.append(cp)

    def landed(dst, s, r):
        pltpu.make_async_remote_copy(
            src_ref=dst, dst_ref=dst, send_sem=s, recv_sem=r, device_id=peers[0], device_id_type=MESH
        ).wait_recv()

    def send_x(d, e):
        push(x_ref.at[batch(plane(d), core(e))], xg.at[:, xcols(c, z, x)],
             x_send.at[d * layers + e], x_recv.at[d * layers + e], dev(y, plane(d), x, core(e)))

    def send_y(d, e):
        push(y_ref.at[batch(plane(d), core(e))], yg.at[d, :, ycols(c, y)],
             y_send.at[d * layers + e], y_recv.at[d * layers + e], dev(y, plane(d), x, core(e)))

    def forward_x(d, e, src=None):
        zone = xg.at[:, xcols(core(-e), plane(-d), x)]
        if src is None:
            landed(zone, x_send.at[d * layers + e], x_recv.at[d * layers + e])
        for j, xx in enumerate(xline):
            i = (d * layers + e) * len(xline) + j
            push(zone if src is None else src, zone, xf_send.at[i], xf_recv.at[i], dev(y, z, xx, c))

    def forward_y(d, e, src=None):
        zone = yg.at[d, :, ycols(core(-e), y)]
        if src is None:
            landed(zone, y_send.at[d * layers + e], y_recv.at[d * layers + e])
        for j, yy in enumerate(yline):
            i = (d * layers + e) * len(yline) + j
            push(zone if src is None else src, zone, yf_send.at[i], yf_recv.at[i], dev(yy, z, x, c))

    mine = batch(z, c)
    forward_x(0, 0, x_ref.at[mine])
    forward_y(0, 0, y_ref.at[mine])
    keep_x = pltpu.make_async_copy(x_ref.at[mine], xg.at[:, xcols(c, z, x)], local_sem.at[0])
    keep_y = pltpu.make_async_copy(y_ref.at[mine], yg.at[0, :, ycols(c, y)], local_sem.at[1])
    keep_x.start()
    keep_y.start()

    far = planes // 2
    near = [d for d in range(1, planes) if not (relayed and d == far)]
    if relayed:
        back = dev(y, plane(-1), x, c)
        push(x_ref.at[batch(plane(far), core(1))], rx, r_send.at[0], r_recv.at[0], back)
        push(y_ref.at[batch(plane(far), core(0))], ry, r_send.at[1], r_recv.at[1], back)
        send_x(far, 0)
        send_y(far, 1)
    for e in range(1, layers):
        send_x(0, e)
        send_y(0, e)
    for d in near:
        send_x(d, 0)
        send_y(d, 0)
    if relayed:
        i = far * layers
        landed(rx, r_send.at[0], r_recv.at[0])
        push(rx, xg.at[:, xcols(c, plane(1), x)], q_send.at[0], x_recv.at[i + 1],
             dev(y, plane(-1), x, core(1)))
        landed(ry, r_send.at[1], r_recv.at[1])
        push(ry, yg.at[far, :, ycols(c, y)], q_send.at[1], y_recv.at[i],
             dev(y, plane(-1), x, c))
    for e in range(1, layers):
        for d in near:
            send_x(d, e)
            send_y(d, e)

    for e in range(1, layers):
        forward_x(0, e)
        forward_y(0, e)
    order = [(d, 0) for d in near]
    if relayed:
        order = [(far, 0, "x"), (far, 1, "y")] + order + [(far, 1, "x"), (far, 0, "y")]
    order += [(d, e) for e in range(1, layers) for d in near]
    for step in order:
        which = step[2] if len(step) > 2 else "xy"
        if "x" in which:
            forward_x(step[0], step[1])
        if "y" in which:
            forward_y(step[0], step[1])

    keep_x.wait()
    keep_y.wait()
    for d in range(planes):
        for e in range(layers):
            for j in range(len(xline)):
                xx = lax.rem(x - (j + 1) + lines, lines)
                i = (d * layers + e) * len(xline) + j
                landed(xg.at[:, xcols(core(-e), plane(-d), xx)], xf_send.at[i], xf_recv.at[i])
    for d in range(planes):
        for e in range(layers):
            for j in range(len(yline)):
                yy = lax.rem(y - (j + 1) + rows, rows)
                i = (d * layers + e) * len(yline) + j
                landed(yg.at[d, :, ycols(core(-e), yy)], yf_send.at[i], yf_recv.at[i])

    tile = min(height, 256)

    def multiply(d, low, high):
        def body(r, _):
            at = pl.ds(pl.multiple_of(r * tile, tile), tile)
            og[d, at, :] = lax.dot_general(
                xg[at, :], yg[d], NT, preferred_element_type=jnp.float32
            ).astype(jnp.bfloat16)
            return 0

        lax.fori_loop(low // tile, high // tile, body, 0)

    top, low_half = pl.ds(0, half), pl.ds(half, half)
    if relayed:
        multiply(far, half, height)
        push(og.at[far, low_half], ro, op_send.at[0], op_recv.at[0], dev(y, plane(-1), x, c))
        multiply(far, 0, half)
        push(og.at[far, top], o_ref.at[z, top], o_send.at[far], o_recv.at[far], dev(y, plane(-far), x, c))
    for d in near:
        multiply(d, 0, height)
        push(og.at[d], o_ref.at[z], o_send.at[d], o_recv.at[d], dev(y, plane(-d), x, c))
    if relayed:
        landed(ro, op_send.at[0], op_recv.at[0])
        push(ro, o_ref.at[plane(1), low_half], oq_send.at[0], op_recv.at[1], dev(y, plane(-1), x, c))
    multiply(0, 0, height)
    keep = pltpu.make_async_copy(og.at[0], o_ref.at[z], local_sem.at[2])
    keep.start()
    for d in near:
        landed(o_ref.at[plane(d)], o_send.at[d], o_recv.at[d])
    if relayed:
        landed(o_ref.at[plane(far), top], o_send.at[far], o_recv.at[far])
        landed(o_ref.at[plane(far), low_half], oq_send.at[0], op_recv.at[1])
    keep.wait()
    for cp in sent:
        cp.wait_send()


def routed(sizes, anomaly_x, anomaly_y):
    rows, planes, lines, layers = sizes
    batches, height, depth_x = anomaly_x.shape
    width, depth_y = anomaly_y.shape[1:]
    members = depth_y * rows * layers
    blocks = planes * layers
    dma = pltpu.SemaphoreType.DMA
    any_ = pl.BlockSpec(memory_space=pl.ANY)
    fx, fy = max(1, blocks * (lines - 1)), max(1, blocks * (rows - 1))
    kind = anomaly_x.dtype
    return pl.pallas_call(
        functools.partial(kernel, sizes),
        out_shape=jax.ShapeDtypeStruct((planes, height, width), jnp.bfloat16),
        in_specs=[any_, any_],
        out_specs=any_,
        scratch_shapes=[
            pltpu.VMEM((height, members), kind),
            pltpu.VMEM((planes, width, members), kind),
            pltpu.VMEM((planes, height, width), jnp.bfloat16),
            pltpu.VMEM((height, depth_x), kind),
            pltpu.VMEM((width, depth_y), kind),
            pltpu.VMEM((height // 2, width), jnp.bfloat16),
            dma((3,)),
            dma((blocks,)), dma((blocks,)), dma((fx,)), dma((fx,)),
            dma((blocks,)), dma((blocks,)), dma((fy,)), dma((fy,)),
            dma((2,)), dma((2,)), dma((2,)),
            dma((planes,)), dma((planes,)), dma((1,)), dma((2,)), dma((1,)),
        ],
        compiler_params=pltpu.CompilerParams(
            collective_id=0, has_side_effects=True, vmem_limit_bytes=60 * 2**20
        ),
    )(anomaly_x, anomaly_y)


def on_device(mesh, anomaly_x, anomaly_y):
    rows, cols, layers = (mesh.shape[name] for name in ("row", "col", "layer"))
    batches, _, depth_x = anomaly_x.shape
    planes = batches // layers
    if layers != 2 or batches % layers or cols % planes or depth_x % LANES:
        return gathered(anomaly_x, anomaly_y)
    return routed((rows, planes, cols // planes, layers), anomaly_x, anomaly_y)


def solution(mesh):
    placed = (P(None, "row", ("layer", "col")), P(None, "col", ("layer", "row")))
    return jax.shard_map(
        functools.partial(on_device, mesh),
        mesh=mesh, in_specs=placed, out_specs=P("layer", "row", "col"), check_vma=False,
    )
```

time: 1590 us -> 630 us (0.40)
  waiting for transfers between devices: 1520 us -> 0 us
  Pallas kernels: 0 us -> 622 us
  matrix products: 49.1 us -> 0 us
    all_gather x2 -> x0, waiting for transfers between devices: 1470 us -> none  [the longest x1 1270 us: on_device(): panel_x = lax.all_gather(anomaly_x, 'col', axis=2, tiled=True)]
    pallas_call x0 -> x1, Pallas kernels: none -> 622 us  [routed(): pl.pallas_call(functools.partial(kernel, sizes), out_shape=jax.ShapeDtype...]
    dot_general x1 -> x0, matrix products: 49.1 us -> none  [on_device(): jnp.einsum('bik,bjk->bij', panel_x, lax.all_gather(anomaly_y, 'row', axis...]
    reduce_scatter x1 -> x0, waiting for transfers between devices: 43.3 us -> none  [on_device(): lax.psum_scatter(partial_tile, 'layer', scatter_dimension=0, tiled=True)]
  transfers between devices with their start and end apart: 3 -> 0, of which waited for: 3 -> 0; matrix products, arithmetic and copies ran while one was open for 0% -> 0% of each run, Pallas kernels for 0% -> 0%
where the time goes in v1:
time: 630 us
  Pallas kernels  622 us (99%)
  local copies, waits for them, and re-layouts  7.32 us (1%)
    pallas_call x1, Pallas kernels, routed(): pl.pallas_call(functools.partial(kernel, sizes), out_shape=jax.ShapeDtype...  622 us

profile of v1, /device:TPU:9, one launch (start us, length us, event | category | flops | bytes accessed | tf_op | source)
XLA Modules:
  0.0 629.6 jit_solution(3132070332084838777)
XLA Ops:
  0.0 622.3 %shard_map.28 = bf16[4,2048,512]{2,1,0:T(8,128)(2,1)} custom-call(bf16[8,2048,256]{2,1,0:T(8,128)(2,1)} %x_ref.1, bf16[8,512,1024]{2,1,0:T(8,128)(2,1)} %y_ref.1), custom_call_target="tpu_custom_call" | custom-call | tf_op jit(solution)/shard_map/pallas_call | solution.py:217
  622.3 7.3 %copy.4 = bf16[4,2048,512]{2,1,0:T(8,128)(2,1)} copy(bf16[4,2048,512]{2,1,0:T(8,128)(2,1)} %shard_map.28) | data formatting | bytes 16777216

commit v2 on v0

v2 whole, which is shorter than its diff:
```python
import functools

import jax
import jax.numpy as jnp
from jax import lax
from jax.experimental import pallas as pl
from jax.experimental.pallas import tpu as pltpu
from jax.sharding import PartitionSpec as P

LANES = 128
HALVES = 2
MESH = pl.DeviceIdType.MESH
NT = (((1,), (1,)), ((), ()))


def gathered(anomaly_x, anomaly_y):
    panel_x = lax.all_gather(anomaly_x, "col", axis=2, tiled=True)
    partial_tile = jnp.einsum(
        "bik,bjk->bij",
        panel_x,
        lax.all_gather(anomaly_y, "row", axis=2, tiled=True),
        preferred_element_type=jnp.float32,
    )
    summed = lax.psum_scatter(partial_tile, "layer", scatter_dimension=0, tiled=True)
    return summed.astype(jnp.bfloat16)


def kernel(
    sizes, x_ref, y_ref, o_ref, xg, yg, og, local_sem,
    x_send, x_recv, xf_send, xf_recv, y_send, y_recv, yf_send, yf_recv, o_send, o_recv,
):
    rows, planes, lines, layers = sizes
    y, col, c = lax.axis_index("row"), lax.axis_index("col"), lax.axis_index("layer")
    z, x = col // lines, lax.rem(col, lines)
    depth_x, depth_y = x_ref.shape[2], y_ref.shape[2]
    height = x_ref.shape[1]
    group = depth_x * planes * lines
    steps = HALVES
    span = planes // HALVES
    q = lax.rem(z, span)
    base = z - q

    def plane(d):
        return lax.rem(z + d + planes, planes)

    def near(d):
        return lax.rem(q + d + span, span)

    def core(e):
        return lax.rem(c + e + layers, layers)

    def dev(yy, zz, xx, cc):
        return {"row": yy, "col": zz * lines + xx, "layer": cc}

    def xcols(cc, zz, xx):
        return pl.ds(pl.multiple_of(cc * group + (zz * lines + xx) * depth_x, depth_x), depth_x)

    def ycols(cc, yy):
        return pl.ds(pl.multiple_of(cc * group + yy * depth_y, depth_y), depth_y)

    def batch(qq, cc, s):
        return cc * planes + qq * steps + s

    xline = [lax.rem(x + d, lines) for d in range(1, lines)]
    yline = [lax.rem(y + d, rows) for d in range(1, rows)]
    peers = [dev(y, plane(d), x, core(e)) for d in range(planes) for e in range(layers) if d or e]
    peers += [dev(y, z, xx, c) for xx in xline] + [dev(yy, z, x, c) for yy in yline]
    barrier = pltpu.get_barrier_semaphore()
    for peer in peers:
        pl.semaphore_signal(barrier, inc=1, device_id=peer, device_id_type=MESH)
    pl.semaphore_wait(barrier, len(peers))

    sent = []

    def push(src, dst, s, r, to):
        cp = pltpu.make_async_remote_copy(
            src_ref=src, dst_ref=dst, send_sem=s, recv_sem=r, device_id=to, device_id_type=MESH
        )
        cp.start()
        sent.append(cp)

    def landed(dst, s, r):
        pltpu.make_async_remote_copy(
            src_ref=dst, dst_ref=dst, send_sem=s, recv_sem=r, device_id=peers[0], device_id_type=MESH
        ).wait_recv()

    def send_x(s, d, e):
        i = (s * planes + d) * layers + e
        to = plane(d)
        push(x_ref.at[batch(lax.rem(to, span), core(e), s)], xg.at[s, :, xcols(c, z, x)],
             x_send.at[i], x_recv.at[i], dev(y, to, x, core(e)))

    def send_y(s, d, e):
        i = (s * span + d) * layers + e
        push(y_ref.at[batch(near(d), core(e), s)], yg.at[s, d, :, ycols(c, y)],
             y_send.at[i], y_recv.at[i], dev(y, base + near(d), x, core(e)))

    def forward_x(s, d, e, src=None):
        i = (s * planes + d) * layers + e
        zone = xg.at[s, :, xcols(core(-e), plane(-d), x)]
        if src is None:
            landed(zone, x_send.at[i], x_recv.at[i])
        for j, xx in enumerate(xline):
            k = i * len(xline) + j
            push(zone if src is None else src, zone, xf_send.at[k], xf_recv.at[k], dev(y, z, xx, c))

    def forward_y(s, d, e, src=None):
        i = (s * span + d) * layers + e
        zone = yg.at[s, d, :, ycols(core(-e), y)]
        if src is None:
            landed(zone, y_send.at[i], y_recv.at[i])
        for j, yy in enumerate(yline):
            k = i * len(yline) + j
            push(zone if src is None else src, zone, yf_send.at[k], yf_recv.at[k], dev(yy, z, x, c))

    far = planes // 2
    order = [(far, e) for e in range(layers)]
    order += [(d, e) for d in range(1, planes) if d != far for e in range(layers)]
    keeps = []
    for s in range(steps):
        own = batch(q, c, s)
        forward_x(s, 0, 0, x_ref.at[own])
        forward_y(s, 0, 0, y_ref.at[own])
        keep_x = pltpu.make_async_copy(x_ref.at[own], xg.at[s, :, xcols(c, z, x)], local_sem.at[2 * s])
        keep_y = pltpu.make_async_copy(y_ref.at[own], yg.at[s, 0, :, ycols(c, y)], local_sem.at[2 * s + 1])
        keep_x.start()
        keep_y.start()
        keeps.append((keep_x, keep_y))
        for e in range(1, layers):
            send_x(s, 0, e)
            send_y(s, 0, e)
        for d, e in order:
            send_x(s, d, e)
            if d < span:
                send_y(s, d, e)

    tile = min(height, 256)

    def multiply(s, d):
        def body(r, _):
            at = pl.ds(pl.multiple_of(r * tile, tile), tile)
            og[s, d, at, :] = lax.dot_general(
                xg[s, at, :], yg[s, d], NT, preferred_element_type=jnp.float32
            ).astype(jnp.bfloat16)
            return 0

        lax.fori_loop(0, height // tile, body, 0)

    outs = []
    for s in range(steps):
        for e in range(1, layers):
            forward_x(s, 0, e)
            forward_y(s, 0, e)
        for d in list(range(1, far)) + list(range(far + 1, planes)) + [far]:
            for e in range(layers):
                forward_x(s, d, e)
                if d < span:
                    forward_y(s, d, e)
        for keep in keeps[s]:
            keep.wait()
        for d in range(planes):
            for e in range(layers):
                for j in range(len(xline)):
                    xx = lax.rem(x - (j + 1) + lines, lines)
                    k = ((s * planes + d) * layers + e) * len(xline) + j
                    landed(xg.at[s, :, xcols(core(-e), plane(-d), xx)], xf_send.at[k], xf_recv.at[k])
        for d in range(span):
            for e in range(layers):
                for j in range(len(yline)):
                    yy = lax.rem(y - (j + 1) + rows, rows)
                    k = ((s * span + d) * layers + e) * len(yline) + j
                    landed(yg.at[s, d, :, ycols(core(-e), yy)], yf_send.at[k], yf_recv.at[k])
        for d in list(range(1, span)):
            multiply(s, d)
            push(og.at[s, d], o_ref.at[q * steps + s], o_send.at[s * span + d], o_recv.at[s * span + d],
                 dev(y, base + near(-d), x, c))
        multiply(s, 0)
        keep = pltpu.make_async_copy(og.at[s, 0], o_ref.at[q * steps + s], local_sem.at[2 * steps + s])
        keep.start()
        outs.append(keep)
    for s in range(steps):
        for d in range(1, span):
            landed(o_ref.at[near(d) * steps + s], o_send.at[s * span + d], o_recv.at[s * span + d])
        outs[s].wait()
    for cp in sent:
        cp.wait_send()


def routed(sizes, anomaly_x, anomaly_y):
    rows, planes, lines, layers = sizes
    _, height, depth_x = anomaly_x.shape
    width, depth_y = anomaly_y.shape[1:]
    members = depth_y * rows * layers
    span, steps = planes // HALVES, HALVES
    bx, by = steps * planes * layers, steps * span * layers
    dma = pltpu.SemaphoreType.DMA
    any_ = pl.BlockSpec(memory_space=pl.ANY)
    fx, fy = max(1, bx * (lines - 1)), max(1, by * (rows - 1))
    kind = anomaly_x.dtype
    return pl.pallas_call(
        functools.partial(kernel, sizes),
        out_shape=jax.ShapeDtypeStruct((planes, height, width), jnp.bfloat16),
        in_specs=[any_, any_],
        out_specs=any_,
        scratch_shapes=[
            pltpu.VMEM((steps, height, members), kind),
            pltpu.VMEM((steps, span, width, members), kind),
            pltpu.VMEM((steps, span, height, width), jnp.bfloat16),
            dma((3 * steps,)),
            dma((bx,)), dma((bx,)), dma((fx,)), dma((fx,)),
            dma((by,)), dma((by,)), dma((fy,)), dma((fy,)),
            dma((steps * span,)), dma((steps * span,)),
        ],
        compiler_params=pltpu.CompilerParams(
            collective_id=0, has_side_effects=True, vmem_limit_bytes=63 * 2**20
        ),
    )(anomaly_x, anomaly_y)


def on_device(mesh, anomaly_x, anomaly_y):
    rows, cols, layers = (mesh.shape[name] for name in ("row", "col", "layer"))
    batches, _, depth_x = anomaly_x.shape
    planes = batches // layers
    if batches % layers or planes % HALVES or cols % planes or depth_x % LANES:
        return gathered(anomaly_x, anomaly_y)
    return routed((rows, planes, cols // planes, layers), anomaly_x, anomaly_y)


def solution(mesh):
    placed = (P(None, "row", ("layer", "col")), P(None, "col", ("layer", "row")))
    return jax.shard_map(
        functools.partial(on_device, mesh),
        mesh=mesh, in_specs=placed, out_specs=P("layer", "row", "col"), check_vma=False,
    )
```

time: 1590 us -> 502 us (0.32)
  waiting for transfers between devices: 1520 us -> 0 us
  Pallas kernels: 0 us -> 492 us
  matrix products: 49.1 us -> 0 us
    all_gather x2 -> x0, waiting for transfers between devices: 1470 us -> none  [the longest x1 1270 us: on_device(): panel_x = lax.all_gather(anomaly_x, 'col', axis=2, tiled=True)]
    pallas_call x0 -> x1, Pallas kernels: none -> 492 us  [routed(): pl.pallas_call(functools.partial(kernel, sizes), out_shape=jax.ShapeDtype...]
    dot_general x1 -> x0, matrix products: 49.1 us -> none  [on_device(): jnp.einsum('bik,bjk->bij', panel_x, lax.all_gather(anomaly_y, 'row', axis...]
    reduce_scatter x1 -> x0, waiting for transfers between devices: 43.3 us -> none  [on_device(): lax.psum_scatter(partial_tile, 'layer', scatter_dimension=0, tiled=True)]
  transfers between devices with their start and end apart: 3 -> 0, of which waited for: 3 -> 0; matrix products, arithmetic and copies ran while one was open for 0% -> 0% of each run, Pallas kernels for 0% -> 0%
where the time goes in v2:
time: 502 us; the launch traced here: 499 us
  Pallas kernels  492 us (98%)
  local copies, waits for them, and re-layouts  7.32 us (1%)
    pallas_call x1, Pallas kernels, routed(): pl.pallas_call(functools.partial(kernel, sizes), out_shape=jax.ShapeDtype...  492 us

profile of v2, /device:TPU:9, one launch (start us, length us, event | category | flops | bytes accessed | tf_op | source)
XLA Modules:
  0.0 499.2 jit_solution(15394165146036573926)
XLA Ops:
  0.0 491.9 %shard_map.28 = bf16[4,2048,512]{2,1,0:T(8,128)(2,1)} custom-call(bf16[8,2048,256]{2,1,0:T(8,128)(2,1)} %x_ref.1, bf16[8,512,1024]{2,1,0:T(8,128)(2,1)} %y_ref.1), custom_call_target="tpu_custom_call" | custom-call | tf_op jit(solution)/shard_map/pallas_call | solution.py:200
  491.9 7.3 %copy.4 = bf16[4,2048,512]{2,1,0:T(8,128)(2,1)} copy(bf16[4,2048,512]{2,1,0:T(8,128)(2,1)} %shard_map.28) | data formatting | bytes 16777216
